TPU v7x, 32 devices: a whole 2x2x4 slice. The times are simulated.
32 devices in a mesh: row: 4 (over y, x), col: 8 (over z, core).
Axes of the slice: x: 2, y: 2, z: 4, core: 2. Of those that a mesh axis runs over, the one named last changes fastest.
Arguments:
- tiles: bfloat16 [4, 8, 128, 128, 128], P('row', 'col'), may hold values from 0 to 0.31
- block_rows: int32 [4, 8, 128], P('row', 'col'), may hold values from 0 to 63, as said below
- block_cols: int32 [4, 8, 128], P('row', 'col'), may hold values from 0 to 127
- counts: int32 [4, 8], P('row', 'col'), may hold values from 1 to 128, as said below
- seeds: int32 [8, 65536], P(None, ('col', 'row')), may hold values from 1 to 999
Outputs:
- vectors_out: float32 [8, 65536], P(None, ('col', 'row'))
- deltas: float32 [4, 8], replicated
Inputs may be any that keep to these rules, and one draw needn't show every extreme that they name: `counts`: each entry is 1, a half, a quarter or an eighth of 128 (at least 1); some device is full in every draw. On each device, among the values of block_rows (over all 128 slots) that share one quotient by 16, at most 4 are distinct; on a device whose count is 128, some quotient has exactly 4 distinct values among its tiles.
All inputs are finite; a program needn't handle non-finite values.
Results may differ from a plain program's by a relative error of at most 0.00061.
Values may be sent and summed in bfloat16 or wider, within the bound.
A program may use at most 64 MiB of HBM per device.

v0:
```python
import jax
import jax.numpy as jnp
from jax import lax
from jax.sharding import PartitionSpec as P

BLOCK = 128
TILE_BLOCK = 32
ITERS = 4
ROW_CAP = 4


def apply_tiles(partial_value, gathered, panel_block, target_block, cols_block, weight):
    taken_rows = gathered[cols_block]
    product = jnp.einsum(
        "tkc,trc->tkr", taken_rows, panel_block, preferred_element_type=jnp.float32
    )
    return partial_value.at[target_block].add(product * weight[:, None, None])


def on_device(tiles, block_rows, block_cols, counts, seeds):
    panels = tiles[0, 0]
    rows_local = block_rows[0, 0]
    cols_local = block_cols[0, 0]
    count_here = counts[0, 0]
    vectors = seeds.shape[0]
    piece_len = seeds.shape[1]
    piece_blocks = piece_len // BLOCK
    row_count = lax.axis_size("row")
    total_nodes = piece_len * row_count * lax.axis_size("col")
    row_span = row_count * piece_blocks
    tile_total = panels.shape[0]
    lane_index = jnp.arange(TILE_BLOCK, dtype=jnp.int32)
    tile_index = jnp.arange(tile_total, dtype=jnp.int32)
    live_flag = tile_index < count_here
    live_mask = live_flag.astype(jnp.float32)
    block_index = jnp.arange(row_span, dtype=jnp.int32)
    hits = (rows_local[None, :] == block_index[:, None]) & live_flag[None, :]
    present = jnp.max(hits.astype(jnp.int32), axis=1).reshape(row_count, piece_blocks)
    rank = jnp.cumsum(present, axis=1) - present
    owner_index = jnp.arange(row_count, dtype=jnp.int32)
    block_slot = (owner_index[:, None] * ROW_CAP + rank).reshape(row_span)
    slot_total = row_count * ROW_CAP
    matched = jnp.where(rows_local[:, None] == block_index[None, :], block_slot[None, :], 0)
    targets = jnp.minimum(jnp.sum(matched, axis=1), slot_total - 1)
    slot_index = jnp.arange(ROW_CAP, dtype=jnp.int32)
    offset_index = jnp.arange(piece_blocks, dtype=jnp.int32)
    matches = (present[:, None, :] == 1) & (rank[:, None, :] == slot_index[None, :, None])
    slot_ids = jnp.sum(jnp.where(matches, offset_index[None, None, :], 0), axis=2)
    row_total = jnp.sum(panels, axis=2, dtype=jnp.float32) * live_mask[:, None]
    degree_part = (
        jnp.zeros((slot_total, 1, BLOCK), jnp.float32).at[targets].add(row_total[:, None, :])
    )
    seed_float = seeds.astype(jnp.float32)
    seed_total = lax.psum(jnp.sum(seed_float, axis=1), ("row", "col"))
    current = (
        (total_nodes * seed_float / seed_total[:, None])
        .reshape(vectors, piece_blocks, BLOCK)
        .transpose(1, 0, 2)
    )
    empty_sum = jnp.zeros((slot_total, vectors, BLOCK), jnp.float32)
    deltas = []
    divisor = None
    owner_table = None
    for iteration in range(ITERS):
        current_half = current.astype(jnp.bfloat16)
        gathered = lax.all_gather(current_half, "col", axis=0, tiled=True)

        def advance(block_at, partial_value):
            begin_at = block_at * TILE_BLOCK
            weight = (begin_at + lane_index < count_here).astype(jnp.float32)
            return apply_tiles(
                partial_value,
                gathered,
                lax.dynamic_slice_in_dim(panels, begin_at, TILE_BLOCK, 0),
                lax.dynamic_slice_in_dim(targets, begin_at, TILE_BLOCK, 0),
                lax.dynamic_slice_in_dim(cols_local, begin_at, TILE_BLOCK, 0),
                weight,
            )

        partial_value = lax.fori_loop(
            0, (count_here + TILE_BLOCK - 1) // TILE_BLOCK, advance, empty_sum
        )
        shaped = partial_value.reshape(row_count, ROW_CAP, vectors, BLOCK)
        if iteration == 0:
            degree_shaped = degree_part.reshape(row_count, ROW_CAP, 1, BLOCK)
            incoming, degree_in, received_ids = (
                lax.all_to_all(shaped, "row", split_axis=0, concat_axis=0, tiled=True),
                lax.all_to_all(degree_shaped, "row", split_axis=0, concat_axis=0, tiled=True),
                lax.all_to_all(slot_ids, "row", split_axis=0, concat_axis=0, tiled=True),
            )
            block_index_own = jnp.arange(piece_blocks, dtype=jnp.int32)
            owner_table = (received_ids.reshape(-1)[None, :] == block_index_own[:, None]).astype(
                jnp.float32
            )
            degree_piece = jnp.dot(
                owner_table,
                degree_in.reshape(row_count * ROW_CAP, BLOCK),
                precision=lax.Precision.HIGHEST,
                preferred_element_type=jnp.float32,
            )
            divisor = 1.0 + degree_piece.reshape(piece_blocks, 1, BLOCK)
        else:
            incoming = lax.all_to_all(shaped, "row", split_axis=0, concat_axis=0, tiled=True)
        summed = jnp.dot(
            owner_table,
            incoming.reshape(row_count * ROW_CAP, vectors * BLOCK),
            precision=lax.Precision.HIGHEST,
            preferred_element_type=jnp.float32,
        ).reshape(piece_blocks, vectors, BLOCK)
        raw_next = (summed + current) / divisor
        local_total = jnp.sum(raw_next, axis=(0, 2))
        totals = lax.psum(local_total, ("row", "col"))
        updated = total_nodes * raw_next / totals[None, :, None]
        deltas.append(lax.pmax(jnp.max(jnp.abs(updated - current), axis=(0, 2)), ("row", "col")))
        current = updated
    vectors_out = current.transpose(1, 0, 2).reshape(vectors, piece_len)
    return (vectors_out, jnp.stack(deltas))


def solution(mesh):
    placed = (
        P("row", "col", None, None, None),
        P("row", "col", None),
        P("row", "col", None),
        P("row", "col"),
        P(None, ("col", "row")),
    )
    return jax.shard_map(
        on_device,
        mesh=mesh,
        in_specs=placed,
        out_specs=(P(None, ("col", "row")), P()),
        check_vma=False,
    )
```

profile of v0, /device:TPU:0, one launch (start us, length us, event | category | flops | bytes accessed | tf_op | source)
XLA Modules:
  0.0 453.3 jit_solution(6785953493534906902)
XLA Ops:
  3.1 5.2 %all-to-all-start = ((s32[4,1,4]{2,1,0:T(1,128)}), s32[4,1,4]{2,1,0:T(1,128)S(1)}, u32[]{:S(2)}, u32[]{:S(2)}) async-start(s32[4,1,4]{2,1,0:T(1,128)} %bitcast.3), calls=%async_computation | async-start | bytes 4096 | tf_op jit(solution)/shard_map/all_to_all | solution.py:89
  10.3 40.9 %psum.35 = f32[8]{0:T(128)S(1)} all-reduce(f32[8]{0:T(128)S(1)} %convert_reduce_fusion.1), channel_id=1, replica_groups=mesh['row'=4,'col'=8] {'row','col'}, use_global_device_ids=true, to_apply=%region_5.6 | all-reduce | flops 8 | bytes 64 | tf_op jit(solution)/shard_map/psum | solution.py:54
  52.2 14.3 %all_gather.12 = bf16[128,8,128]{2,0,1:T(8,128)(2,1)S(1)} all-gather(bf16[16,8,128]{2,0,1:T(8,128)(2,1)S(1)} %bitcast.214), channel_id=1, replica_groups=mesh['row'=4,'col'=8] {'col'}, dimensions={0}, use_global_device_ids=true | all-gather | bytes 294912 | tf_op jit(solution)/shard_map/all_gather | solution.py:66
  71.6 3.6 all-to-all-start.2
  75.8 28.4 %while.44 = (s32[]{:T(128)}, f32[16,8,128]{2,1,0:T(8,128)}, s32[]{:T(128)}, s32[128]{0:T(128)S(1)}, s32[128]{0:T(128)S(1)}, /*index=5*/bf16[128,8,128]{2,1,0:T(8...) while((s32[]{:T(128)}, f32[16,8,128]{2,1,0:T(8,128)}, ...), condition=%wide.region_8.9_spmd.clone, body=%wide.region_6.8_spmd.clone.sunk | while | flops 8455462 | bytes 1774899 | solution.py:80
  79.0 3.9 scatter_fusion
  86.1 3.9 scatter_fusion
  93.2 3.9 scatter_fusion
  100.3 3.9 scatter_fusion
  108.9 4.7 %all-to-all-done.1 = f32[4,4,8,128]{3,2,1,0:T(8,128)S(1)} async-done(((f32[4,4,8,128]{3,2,1,0:T(8,128)}), f32[4,4,8,128]{3,2,1,0:T(8,128)S(1)}, u32[]{:S(2)}, u32[]{:S(2)}) %all-to-all-start.1) | async-done | bytes 65568 | tf_op jit(solution)/shard_map/all_to_all | solution.py:87
  113.9 38.1 %psum.36 = f32[8]{0:T(128)S(1)} all-reduce(f32[8]{0:T(128)S(1)} %get-tuple-element.490), channel_id=1, replica_groups=mesh['row'=4,'col'=8] {'row','col'}, use_global_device_ids=true, to_apply=%region_12.13 | all-reduce | flops 8 | bytes 64 | tf_op jit(solution)/shard_map/psum | solution.py:112
  152.1 14.2 %all_gather.13 = bf16[128,8,128]{2,0,1:T(8,128)(2,1)S(1)} all-gather(bf16[16,8,128]{2,0,1:T(8,128)(2,1)S(1)} %get-tuple-element.480), channel_id=1, replica_groups=mesh['row'=4,'col'=8] {'col'}, dimensions={0}, use_global_device_ids=true | all-gather | bytes 294912 | tf_op jit(solution)/shard_map/all_gather | solution.py:66
  167.1 28.4 %while.45 = (s32[]{:T(128)}, f32[16,8,128]{2,1,0:T(8,128)}, s32[]{:T(128)}, s32[128]{0:T(128)S(1)}, s32[128]{0:T(128)S(1)}, /*index=5*/bf16[128,8,128]{2,1,0:T(8...) while((s32[]{:T(128)}, f32[16,8,128]{2,1,0:T(8,128)}, ...), condition=%wide.region_15.16_spmd.clone, body=%wide.region_13.15_spmd.clone.sunk | while | flops 8455462 | bytes 1774899 | solution.py:80
  170.3 3.9 scatter_fusion.1
  177.4 3.9 scatter_fusion.1
  184.5 3.9 scatter_fusion.1
  191.6 3.9 scatter_fusion.1
  198.8 4.8 %all-to-all-done.3 = f32[4,4,8,128]{3,2,1,0:T(8,128)S(1)} async-done(((f32[4,4,8,128]{3,2,1,0:T(8,128)}), f32[4,4,8,128]{3,2,1,0:T(8,128)S(1)}, u32[]{:S(2)}, u32[]{:S(2)}) %all-to-all-start.3) | async-done | bytes 65568 | tf_op jit(solution)/shard_map/all_to_all | solution.py:103
  203.9 37.7 %psum.37 = f32[8]{0:T(128)S(1)} all-reduce(f32[8]{0:T(128)S(1)} %get-tuple-element.403), channel_id=1, replica_groups=mesh['row'=4,'col'=8] {'row','col'}, use_global_device_ids=true, to_apply=%region_17.18 | all-reduce | flops 8 | bytes 64 | tf_op jit(solution)/shard_map/psum | solution.py:112
  241.7 14.3 %all_gather.14 = bf16[128,8,128]{2,0,1:T(8,128)(2,1)S(1)} all-gather(bf16[16,8,128]{2,0,1:T(8,128)(2,1)S(1)} %get-tuple-element.478), channel_id=1, replica_groups=mesh['row'=4,'col'=8] {'col'}, dimensions={0}, use_global_device_ids=true | all-gather | bytes 294912 | tf_op jit(solution)/shard_map/all_gather | solution.py:66
  256.8 28.4 %while.46 = (s32[]{:T(128)}, f32[16,8,128]{2,1,0:T(8,128)}, s32[]{:T(128)}, s32[128]{0:T(128)S(1)}, s32[128]{0:T(128)S(1)}, /*index=5*/bf16[128,8,128]{2,1,0:T(8...) while((s32[]{:T(128)}, f32[16,8,128]{2,1,0:T(8,128)}, ...), condition=%wide.region_20.21_spmd.clone, body=%wide.region_18.20_spmd.clone.sunk | while | flops 8455462 | bytes 1774899 | solution.py:80
  260.0 3.9 scatter_fusion.2
  267.1 3.9 scatter_fusion.2
  274.2 3.9 scatter_fusion.2
  281.2 3.9 scatter_fusion.2
  288.4 4.8 %all-to-all-done.4 = f32[4,4,8,128]{3,2,1,0:T(8,128)S(1)} async-done(((f32[4,4,8,128]{3,2,1,0:T(8,128)}), f32[4,4,8,128]{3,2,1,0:T(8,128)S(1)}, u32[]{:S(2)}, u32[]{:S(2)}) %all-to-all-start.4) | async-done | bytes 65568 | tf_op jit(solution)/shard_map/all_to_all | solution.py:103
  293.5 38.1 %psum.38 = f32[8]{0:T(128)S(1)} all-reduce(f32[8]{0:T(128)S(1)} %get-tuple-element.405), channel_id=1, replica_groups=mesh['row'=4,'col'=8] {'row','col'}, use_global_device_ids=true, to_apply=%region_22.23 | all-reduce | flops 8 | bytes 64 | tf_op jit(solution)/shard_map/psum | solution.py:112
  331.7 14.4 %all_gather.15 = bf16[128,8,128]{2,0,1:T(8,128)(2,1)S(1)} all-gather(bf16[16,8,128]{2,0,1:T(8,128)(2,1)S(1)} %get-tuple-element.476), channel_id=1, replica_groups=mesh['row'=4,'col'=8] {'col'}, dimensions={0}, use_global_device_ids=true | all-gather | bytes 294912 | tf_op jit(solution)/shard_map/all_gather | solution.py:66
  346.3 19.7 %while.47 = (s32[]{:T(128)}, f32[16,8,128]{2,1,0:T(8,128)S(1)}, s32[]{:T(128)}, s32[128]{0:T(128)S(1)}, s32[128]{0:T(128)S(1)}, /*index=5*/bf16[128,8,128]{2,1,0...) while((s32[]{:T(128)}, f32[16,8,128]{2,1,0:T(8,128)S(1)}, ...), condition=%wide.region_25.26_spmd.clone, body=%wide.region_23.25_spmd.clone.sunk | while | flops 8455462 | bytes 1774899 | solution.py:80
  365.9 7.2 %all_to_all.34 = f32[4,4,8,128]{3,2,1,0:T(8,128)S(1)} all-to-all(f32[4,4,8,128]{3,2,1,0:T(8,128)S(1)} %bitcast.212), channel_id=1, replica_groups=mesh['row'=4,'col'=8] {'row'}, dimensions={0} | all-to-all | bytes 131072 | tf_op jit(solution)/shard_map/all_to_all | solution.py:103
  373.4 38.5 %psum.39 = f32[8]{0:T(128)S(1)} all-reduce(f32[8]{0:T(128)S(1)} %get-tuple-element.494), channel_id=1, replica_groups=mesh['row'=4,'col'=8] {'row','col'}, use_global_device_ids=true, to_apply=%region_27.28 | all-reduce | flops 8 | bytes 64 | tf_op jit(solution)/shard_map/psum | solution.py:112
  412.9 39.9 %all-reduce = (f32[1,8]{1,0:T(1,128)S(1)}, f32[1,8]{1,0:T(1,128)S(1)}, f32[1,8]{1,0:T(1,128)S(1)}, f32[1,8]{1,0:T(1,128)S(1)}) all-reduce(f32[1,8]{1,0:T(1,128)S(1)} %bitcast.222, f32[1,8]{1,0:T(1,128)S(1)} %bitcast.221, f32[1,8]{1,0:T(1,128)S(1)} %bitcast.224, f32[1,8]{1,0:T(1,128)S(1)} %bitcast.223), channel_id=1, replica_groups=mesh['row'=4,'col'=8] {'row','col'}, use_global_device_ids=true, to_apply=%region_35.36 | all-reduce | flops 32 | bytes 256 | tf_op jit(solution)/shard_map/pmax | solution.py:114
  (134 shorter events, 84.2 us)
Async XLA Ops:
  0.6 75.2 %copy-start = (s32[1,1,128]{2,1,0:T(1,128)S(1)}, s32[1,1,128]{2,1,0:T(1,128)}, u32[]{:S(2)}) copy-start(s32[1,1,128]{2,1,0:T(1,128)} %param.15) | copy-start | bytes 1540
  3.1 68.5 %all-to-all-start = ((s32[4,1,4]{2,1,0:T(1,128)}), s32[4,1,4]{2,1,0:T(1,128)S(1)}, u32[]{:S(2)}, u32[]{:S(2)}) async-start(s32[4,1,4]{2,1,0:T(1,128)} %bitcast.3), calls=%async_computation | async-start | bytes 4096 | tf_op jit(solution)/shard_map/all_to_all | solution.py:89
  71.6 33.8 %all-to-all-start.2 = ((f32[4,4,1,128]{3,1,2,0:T(4,128)}), f32[4,4,1,128]{3,1,2,0:T(4,128)S(1)}, u32[]{:S(2)}, u32[]{:S(2)}) async-start(f32[4,4,1,128]{3,1,2,0:T(4,128)} %bitcast.14), calls=%async_computation.2 | async-start | bytes 16384 | tf_op jit(solution)/shard_map/all_to_all | solution.py:88
  105.5 8.1 %all-to-all-start.1 = ((f32[4,4,8,128]{3,2,1,0:T(8,128)}), f32[4,4,8,128]{3,2,1,0:T(8,128)S(1)}, u32[]{:S(2)}, u32[]{:S(2)}) async-start(f32[4,4,8,128]{3,2,1,0:T(8,128)} %bitcast.8), calls=%async_computation.1 | async-start | bytes 131072 | tf_op jit(solution)/shard_map/all_to_all | solution.py:87
  195.5 8.1 %all-to-all-start.3 = ((f32[4,4,8,128]{3,2,1,0:T(8,128)}), f32[4,4,8,128]{3,2,1,0:T(8,128)S(1)}, u32[]{:S(2)}, u32[]{:S(2)}) async-start(f32[4,4,8,128]{3,2,1,0:T(8,128)} %bitcast.16), calls=%async_computation.3 | async-start | bytes 131072 | tf_op jit(solution)/shard_map/all_to_all | solution.py:103
  285.1 8.1 %all-to-all-start.4 = ((f32[4,4,8,128]{3,2,1,0:T(8,128)}), f32[4,4,8,128]{3,2,1,0:T(8,128)S(1)}, u32[]{:S(2)}, u32[]{:S(2)}) async-start(f32[4,4,8,128]{3,2,1,0:T(8,128)} %bitcast.18), calls=%async_computation.4 | async-start | bytes 131072 | tf_op jit(solution)/shard_map/all_to_all | solution.py:103
where the time goes:
time: 458 us; the launch traced here: 453 us
  blocking collectives  298 us (65%)
  other arithmetic  76.4 us (17%)
  matrix products  31 us (7%)
  starting transfers between devices  18.6 us (4%)
  waiting for transfers between devices  14.3 us (3%)
  local copies, waits for them, and re-layouts  13.7 us (3%)
    psum x4, blocking collectives, on_device(): totals = lax.psum(local_total, ('row', 'col'))  152 us
    all_gather x4, blocking collectives, on_device(): gathered = lax.all_gather(current_half, 'col', axis=0, tiled=True)  57.2 us
    scatter-add x16, other arithmetic, apply_tiles(): return partial_value.at[target_block].add(product * weight[:, None, None])  53.5 us
    psum x1, blocking collectives, on_device(): seed_total = lax.psum(jnp.sum(seed_float, axis=1), ('row', 'col'))  40.9 us
    pmax x1, blocking collectives, on_device(): lax.pmax(jnp.max(jnp.abs(updated - current), axis=(0, 2)), ('row', 'col'))  39.9 us
    dot_general x16, matrix products, apply_tiles(): jnp.einsum('tkc,trc->tkr', taken_rows, panel_block, preferred_element_typ...  29.7 us
    all_to_all x3, waiting for transfers between devices, on_device(): lax.all_to_all(shaped, 'row', split_axis=0, concat_axis=0, tiled=True)  14.3 us
    convert_element_type x16, other arithmetic, advance(): weight = (begin_at + lane_index < count_here).astype(jnp.float32)  10.4 us
  transfers between devices with their start and end apart: 5, of which 3 were waited for; matrix products, arithmetic and copies ran while one was open for 8% of the time, Pallas kernels for 0%

commit v1 on v0

v1 whole, which is shorter than its diff:
```python
import functools

import jax
import jax.numpy as jnp
from jax import lax
from jax.experimental import pallas as pl
from jax.experimental.pallas import tpu as pltpu
from jax.sharding import PartitionSpec as P

BLOCK = 128
ITERS = 4
ROW_CAP = 4
CHUNK = 16
STEP = 4
MESH = pl.DeviceIdType.MESH


def kernel(
    n_row,
    n_col,
    total_nodes,
    targets,
    cols,
    slot_ids,
    tiles,
    seeds,
    out,
    deltas_out,
    panel,
    gath,
    table,
    hist,
    inv_deg,
    part,
    landed,
    deg_send,
    deg_recv,
    tot_send,
    tot_recv,
    tile_sem,
    gs_sem,
    gr_sem,
    rs_sem,
    rr_sem,
    ds_sem,
    dr_sem,
    ts_sem,
    tr_sem,
):
    vectors = seeds.shape[0]
    piece_blocks = seeds.shape[1] // BLOCK
    devices = n_row * n_col
    chips = n_col // 2
    slots = n_row * ROW_CAP
    chunks = panel.shape[0]
    row = lax.axis_index("row")
    col = lax.axis_index("col")
    me = row * n_col + col
    z = col // 2
    core = col % 2
    partner = z * 2 + (1 - core)

    def tile_copy(chunk, t):
        return pltpu.make_async_copy(
            tiles.at[0, 0, chunk * CHUNK + t],
            panel.at[chunk, :, pl.ds(t * BLOCK, BLOCK)],
            tile_sem.at[chunk],
        )

    def start_tiles(chunk, carry):
        for t in range(CHUNK):
            tile_copy(chunk, t).start()
        return carry

    lax.fori_loop(0, chunks, start_tiles, 0)

    barrier = pltpu.get_barrier_semaphore()

    def greet(d, carry):
        f = lax.rem(me + d, devices)
        pl.semaphore_signal(
            barrier, inc=1, device_id=(f // n_col, f % n_col), device_id_type=MESH
        )
        return carry

    lax.fori_loop(1, devices, greet, 0)

    lane = lax.broadcasted_iota(jnp.int32, (vectors, BLOCK), 1)
    sub = lax.broadcasted_iota(jnp.int32, (vectors, BLOCK), 0)

    def to_row(value, base=0):
        return jnp.sum(jnp.where(lane == sub + base, value, 0.0), axis=0, keepdims=True)

    def to_column(value):
        return jnp.sum(jnp.where(lane == sub, value, 0.0), axis=1, keepdims=True)

    def exchange_copy(which, d):
        f = lax.rem(me + d, devices)
        return pltpu.make_async_remote_copy(
            src_ref=tot_send.at[which],
            dst_ref=tot_recv.at[which, d],
            send_sem=ts_sem.at[which],
            recv_sem=tr_sem.at[which],
            device_id=(f // n_col, f % n_col),
            device_id_type=MESH,
        )

    def share(which, value):
        tot_send[which] = value
        tot_recv[which, 0] = value

        def go(d, carry):
            exchange_copy(which, d).start()
            return carry

        lax.fori_loop(1, devices, go, 0)

    def shared(which):
        rest = tot_recv.at[which, pl.ds(1, devices - 1)]
        pltpu.make_async_copy(rest, rest, tr_sem.at[which]).wait()
        return tot_recv[which]

    seed_sum = jnp.zeros((vectors, BLOCK), jnp.float32)
    for b in range(piece_blocks):
        value = seeds[:, b * BLOCK : (b + 1) * BLOCK].astype(jnp.float32)
        hist[0, b] = value
        seed_sum = seed_sum + value
    pl.semaphore_wait(barrier, devices - 1)
    share(0, to_row(jnp.sum(seed_sum, axis=1, keepdims=True)))

    slot_row = lax.broadcasted_iota(jnp.int32, (slots, BLOCK), 0)

    def degree_chunk(chunk, acc):
        pltpu.make_async_copy(panel.at[chunk], panel.at[chunk], tile_sem.at[chunk]).wait()
        pieces = []
        for t in range(CHUNK):
            hit = slot_row == targets[chunk * CHUNK + t]
            pieces.append(jnp.where(hit, 1.0, 0.0).astype(jnp.bfloat16))
        return acc + lax.dot_general(
            jnp.concatenate(pieces, axis=1),
            panel[chunk],
            (((1,), (1,)), ((), ())),
            preferred_element_type=jnp.float32,
        )

    degree = lax.fori_loop(0, chunks, degree_chunk, jnp.zeros((slots, BLOCK), jnp.float32))
    for o in range(n_row):
        ids = [
            jnp.full((1, BLOCK), slot_ids[o * ROW_CAP + s], jnp.int32).astype(jnp.float32)
            for s in range(ROW_CAP)
        ]
        deg_send[o] = jnp.concatenate([degree[o * ROW_CAP : (o + 1) * ROW_CAP]] + ids, axis=0)

    def degree_copy(d):
        to = lax.rem(row + d, n_row)
        return pltpu.make_async_remote_copy(
            src_ref=deg_send.at[to],
            dst_ref=deg_recv.at[row],
            send_sem=ds_sem.at[d],
            recv_sem=dr_sem.at[d],
            device_id=(to, col),
            device_id_type=MESH,
        )

    for d in range(1, n_row):
        degree_copy(d).start()
    deg_recv[row] = deg_send[row]

    def own_copy(it):
        own = gath.at[it, pl.ds(col * piece_blocks, piece_blocks)]
        return pltpu.make_async_remote_copy(
            src_ref=hist.at[it],
            dst_ref=own,
            send_sem=gs_sem.at[it, 0],
            recv_sem=gr_sem.at[it, 0],
            device_id=(row, partner),
            device_id_type=MESH,
        )

    def far_copy(it, d):
        to = lax.rem(z + d, chips) * 2 + core
        own = gath.at[it, pl.ds(col * piece_blocks, piece_blocks)]
        return pltpu.make_async_remote_copy(
            src_ref=hist.at[it],
            dst_ref=own,
            send_sem=gs_sem.at[it, d],
            recv_sem=gr_sem.at[it, d],
            device_id=(row, to),
            device_id_type=MESH,
        )

    def pass_copy(it, d):
        source = lax.rem(z - d + chips, chips) * 2 + core
        there = gath.at[it, pl.ds(source * piece_blocks, piece_blocks)]
        return pltpu.make_async_remote_copy(
            src_ref=there,
            dst_ref=there,
            send_sem=gs_sem.at[it, chips - 1 + d],
            recv_sem=gr_sem.at[it, chips - 1 + d],
            device_id=(row, partner),
            device_id_type=MESH,
        )

    def part_copy(it, d):
        to = lax.rem(row + d, n_row)
        return pltpu.make_async_remote_copy(
            src_ref=part.at[it, to],
            dst_ref=landed.at[it, row],
            send_sem=rs_sem.at[it, d],
            recv_sem=rr_sem.at[it, d],
            device_id=(to, col),
            device_id_type=MESH,
        )

    slot_of_row = (
        lax.broadcasted_iota(jnp.int32, (slots * vectors, BLOCK), 0) // vectors
    ).astype(jnp.float32).astype(jnp.bfloat16)

    def fill_table(it, scale, b):
        value = gath[it, b] * scale
        table[b] = jnp.concatenate([value, value], axis=0).astype(jnp.bfloat16)

    def product_chunk(chunk, acc):
        for g in range(CHUNK // STEP):
            pieces = []
            for s in range(STEP):
                t = g * STEP + s
                at = chunk * CHUNK + t
                taken = table[cols[at]]
                wide = jnp.concatenate([taken] * (slots * vectors // (2 * vectors)), axis=0)
                mine = jnp.full((slots * vectors, BLOCK), targets[at], jnp.int32)
                mine = mine.astype(jnp.float32).astype(jnp.bfloat16)
                pieces.append(jnp.where(slot_of_row == mine, wide, jnp.zeros_like(wide)))
            acc = acc + lax.dot_general(
                jnp.concatenate(pieces, axis=1),
                panel[chunk, :, g * STEP * BLOCK : (g + 1) * STEP * BLOCK],
                (((1,), (1,)), ((), ())),
                preferred_element_type=jnp.float32,
            )
        return acc

    def own_delta(it, scale, scale_before):
        worst = jnp.zeros((vectors, BLOCK), jnp.float32)
        for b in range(piece_blocks):
            change = hist[it + 1, b] * scale - hist[it, b] * scale_before
            worst = jnp.maximum(worst, jnp.abs(change))
        return to_row(jnp.max(worst, axis=1, keepdims=True), it * vectors)

    delta_row = jnp.zeros((1, BLOCK), jnp.float32)
    scale_before = None
    for it in range(ITERS):
        for d in range(1, chips):
            far_copy(it, d).start()
        own_copy(it).start()
        gath[it, pl.ds(col * piece_blocks, piece_blocks)] = hist[it]
        scale = total_nodes / to_column(jnp.sum(shared(it), axis=0))
        if it > 0:
            delta_row = delta_row + own_delta(it - 1, scale, scale_before)
        scale_before = scale
        for d in range(1, chips):
            far_copy(it, d).wait_recv()
            pass_copy(it, d).start()
        own_copy(it).wait_recv()
        for d in range(1, chips):
            pass_copy(it, d).wait_recv()

        @pl.loop(0, gath.shape[1], unroll=8)
        def _(b, it=it, scale=scale):
            fill_table(it, scale, b)

        acc = lax.fori_loop(
            0, chunks, product_chunk, jnp.zeros((slots * vectors, BLOCK), jnp.float32)
        )
        part[it] = acc.reshape(n_row, ROW_CAP * vectors, BLOCK)
        for d in range(1, n_row):
            part_copy(it, d).start()
        landed[it, row] = part[it, row]
        if it == 0:
            for d in range(1, n_row):
                degree_copy(d).wait_recv()
            for p in range(piece_blocks):
                found = jnp.ones((1, BLOCK), jnp.float32)
                for j in range(n_row):
                    for s in range(ROW_CAP):
                        where_to = deg_recv[j, ROW_CAP + s : ROW_CAP + s + 1]
                        found = found + jnp.where(
                            where_to == float(p), deg_recv[j, s : s + 1], 0.0
                        )
                inv_deg[p] = jnp.broadcast_to(1.0 / found, (vectors, BLOCK))
        for d in range(1, n_row):
            part_copy(it, d).wait_recv()
        sums = [hist[it, p] * scale for p in range(piece_blocks)]
        for j in range(n_row):
            for s in range(ROW_CAP):
                value = landed[it, j, s * vectors : (s + 1) * vectors]
                where_to = jnp.broadcast_to(
                    deg_recv[j, ROW_CAP + s : ROW_CAP + s + 1], (vectors, BLOCK)
                )
                for p in range(piece_blocks):
                    sums[p] = sums[p] + jnp.where(where_to == float(p), value, 0.0)
        local = jnp.zeros((vectors, BLOCK), jnp.float32)
        for p in range(piece_blocks):
            fresh = sums[p] * inv_deg[p]
            hist[it + 1, p] = fresh
            local = local + fresh
        share(it + 1, to_row(jnp.sum(local, axis=1, keepdims=True)))

    scale = total_nodes / to_column(jnp.sum(shared(ITERS), axis=0))
    delta_row = delta_row + own_delta(ITERS - 1, scale, scale_before)
    share(ITERS + 1, delta_row)
    for b in range(piece_blocks):
        out[:, b * BLOCK : (b + 1) * BLOCK] = hist[ITERS, b] * scale
    for d in range(1, n_row):
        degree_copy(d).wait_send()
    for it in range(ITERS):
        own_copy(it).wait_send()
        for d in range(1, chips):
            far_copy(it, d).wait_send()
            pass_copy(it, d).wait_send()
        for d in range(1, n_row):
            part_copy(it, d).wait_send()
    top = jnp.max(shared(ITERS + 1), axis=0)
    for n in range(ITERS):
        deltas_out[n : n + 1, :] = top[:, n * vectors : (n + 1) * vectors]
    for which in range(ITERS + 2):
        rest = tot_recv.at[which, pl.ds(1, devices - 1)]
        pltpu.make_async_copy(rest, rest, ts_sem.at[which]).wait()


def on_device(tiles, block_rows, block_cols, counts, seeds):
    n_row = lax.axis_size("row")
    n_col = lax.axis_size("col")
    vectors = seeds.shape[0]
    piece_blocks = seeds.shape[1] // BLOCK
    tile_total = tiles.shape[2]
    slots = n_row * ROW_CAP
    span = n_row * piece_blocks
    chunks = tile_total // CHUNK
    devices = n_row * n_col
    rows = block_rows[0, 0]
    live = jnp.arange(tile_total, dtype=jnp.int32) < counts[0, 0]
    blocks = jnp.arange(span, dtype=jnp.int32)
    hits = (rows[None, :] == blocks[:, None]) & live[None, :]
    present = jnp.max(hits.astype(jnp.int32), axis=1)
    earlier = (blocks[None, :] < blocks[:, None]) & (
        blocks[None, :] // piece_blocks == blocks[:, None] // piece_blocks
    )
    rank = jnp.sum(jnp.where(earlier, present[None, :], 0), axis=1)
    slot = (blocks // piece_blocks) * ROW_CAP + rank
    targets = jnp.sum(jnp.where(hits, slot[:, None] + 1, 0), axis=0) - 1
    slot_index = jnp.arange(slots, dtype=jnp.int32)
    match = (slot[:, None] == slot_index[None, :]) & (present[:, None] == 1)
    slot_ids = jnp.sum(jnp.where(match, (blocks % piece_blocks)[:, None], 0), axis=0)

    smem = pl.BlockSpec(memory_space=pltpu.SMEM)
    vmem = pl.BlockSpec(memory_space=pltpu.VMEM)
    f32, bf16 = jnp.float32, jnp.bfloat16
    dma = pltpu.SemaphoreType.DMA
    out, deltas = pl.pallas_call(
        functools.partial(kernel, n_row, n_col, float(seeds.shape[1] * devices)),
        out_shape=(
            jax.ShapeDtypeStruct(seeds.shape, f32),
            jax.ShapeDtypeStruct((ITERS, vectors), f32),
        ),
        in_specs=[smem, smem, smem, pl.BlockSpec(memory_space=pl.ANY), vmem],
        out_specs=(vmem, vmem),
        scratch_shapes=[
            pltpu.VMEM((chunks, BLOCK, CHUNK * BLOCK), bf16),
            pltpu.VMEM((ITERS, n_col * piece_blocks, vectors, BLOCK), f32),
            pltpu.VMEM((n_col * piece_blocks, 2 * vectors, BLOCK), bf16),
            pltpu.VMEM((ITERS + 1, piece_blocks, vectors, BLOCK), f32),
            pltpu.VMEM((piece_blocks, vectors, BLOCK), f32),
            pltpu.VMEM((ITERS, n_row, ROW_CAP * vectors, BLOCK), f32),
            pltpu.VMEM((ITERS, n_row, ROW_CAP * vectors, BLOCK), f32),
            pltpu.VMEM((n_row, 2 * ROW_CAP, BLOCK), f32),
            pltpu.VMEM((n_row, 2 * ROW_CAP, BLOCK), f32),
            pltpu.VMEM((ITERS + 2, 1, BLOCK), f32),
            pltpu.VMEM((ITERS + 2, devices, 1, BLOCK), f32),
            dma((chunks,)),
            dma((ITERS, n_col)),
            dma((ITERS, n_col)),
            dma((ITERS, n_row)),
            dma((ITERS, n_row)),
            dma((n_row,)),
            dma((n_row,)),
            dma((ITERS + 2,)),
            dma((ITERS + 2,)),
        ],
        compiler_params=pltpu.CompilerParams(collective_id=0, has_side_effects=True),
    )(targets, block_cols[0, 0], slot_ids, tiles, seeds)
    return out, deltas


def solution(mesh):
    placed = (
        P("row", "col", None, None, None),
        P("row", "col", None),
        P("row", "col", None),
        P("row", "col"),
        P(None, ("col", "row")),
    )
    return jax.shard_map(
        on_device,
        mesh=mesh,
        in_specs=placed,
        out_specs=(P(None, ("col", "row")), P()),
        check_vma=False,
    )
```

time: 458 us -> 86.4 us (0.19); the launches traced: 453 us -> 86.3 us
  blocking collectives: 298 us -> 0 us
  Pallas kernels: 0 us -> 79.5 us
  other arithmetic: 76.4 us -> 2.87 us
  matrix products: 31 us -> 0 us
  starting transfers between devices: 18.6 us -> 0 us
  waiting for transfers between devices: 14.3 us -> 0 us
  local copies, waits for them, and re-layouts: 13.7 us -> 2.71 us
    psum x5 -> x0, blocking collectives: 193 us -> none  [the longest x4 152 us: on_device(): totals = lax.psum(local_total, ('row', 'col'))]
    pallas_call x0 -> x1, Pallas kernels: none -> 79.5 us  [on_device(): pl.pallas_call(functools.partial(kernel, n_row, n_col, float(seeds.shape[...]
    all_gather x4 -> x0, blocking collectives: 57.2 us -> none  [on_device(): gathered = lax.all_gather(current_half, 'col', axis=0, tiled=True)]
    scatter-add x17 -> x0, other arithmetic: 55.1 us -> none  [the longest x16 53.5 us: apply_tiles(): return partial_value.at[target_block].add(product * weight[:, None, None])]
    pmax x1 -> x0, blocking collectives: 39.9 us -> none  [on_device(): lax.pmax(jnp.max(jnp.abs(updated - current), axis=(0, 2)), ('row', 'col'))]
    dot_general x21 -> x0, matrix products: 31 us -> none  [the longest x16 29.7 us: apply_tiles(): jnp.einsum('tkc,trc->tkr', taken_rows, panel_block, preferred_element_typ...]
    all_to_all x5 -> x0, starting transfers between devices: 18.6 us -> none  [the longest x3 9.86 us: on_device(): lax.all_to_all(shaped, 'row', split_axis=0, concat_axis=0, tiled=True)]
    all_to_all x5 -> x0, waiting for transfers between devices: 14.3 us -> none  [the longest x3 14.3 us: on_device(): lax.all_to_all(shaped, 'row', split_axis=0, concat_axis=0, tiled=True)]
  transfers between devices with their start and end apart: 5 -> 0, of which waited for: 3 -> 0; matrix products, arithmetic and copies ran while one was open for 8% -> 0% of each run, Pallas kernels for 0% -> 0%
where the time goes in v1:
time: 86.4 us; the launch traced here: 86.3 us
  Pallas kernels  79.5 us (92%)
  other arithmetic  2.87 us (3%)
  local copies, waits for them, and re-layouts  2.71 us (3%)
  between operations  1.32 us (2%)
    pallas_call x1, Pallas kernels, on_device(): pl.pallas_call(functools.partial(kernel, n_row, n_col, float(seeds.shape[...  79.5 us
    unnamed x2, local copies, waits for them, and re-layouts  2.71 us

profile of v1, /device:TPU:0, one launch (start us, length us, event | category | flops | bytes accessed | tf_op | source)
XLA Modules:
  0.0 86.3 jit_solution(7905188382251803463)
XLA Ops:
  1.3 0.8 convert_reduce_fusion
  2.1 0.2 select_reduce_fusion.1
  2.3 0.6 select_reduce_fusion.2.slot_ids
  2.9 0.7 select_reduce_fusion
  3.7 0.5 broadcast_add_fusion.targets
  4.2 79.5 %shard_map.68 = (f32[8,2048]{1,0:T(8,128)}, f32[4,8]{1,0:T(4,128)}) custom-call(s32[128]{0:T(128)} %broadcast_add_fusion.targets, s32[128]{0:T(128)} %bitcast.4, s32[16]{0:T(128)} %select_reduce_fusion.2.slot_ids, bf16[1,1,128,128,128]{4,3,2,1,0:T(8,128)(2,1)} %tiles.1, s32[8,2048]{1,0:T(8,128)} %seeds.1), custom_call_target="tpu_custom_call" | custom-call | tf_op jit(solution)/shard_map/pallas_call | solution.py:359
  83.6 1.5 %copy.10 = f32[8,2048]{1,0:T(8,128)} copy(f32[8,2048]{1,0:T(8,128)} %get-tuple-element.7) | data formatting | bytes 131072
  85.1 1.2 %copy.11 = f32[4,8]{1,0:T(4,128)} copy(f32[4,8]{1,0:T(4,128)} %get-tuple-element.8) | data formatting | bytes 256
  (4 shorter events, 0.0 us)

commit v2 on v1

--- a/solution.py
+++ b/solution.py
@@ -10,6 +10,7 @@
 BLOCK = 128
 ITERS = 4
 ROW_CAP = 4
+RAW_ITERS = 2
 CHUNK = 16
 STEP = 4
 MESH = pl.DeviceIdType.MESH
@@ -22,12 +23,16 @@
     targets,
     cols,
     slot_ids,
+    rows,
+    live_cols,
     tiles,
     seeds,
     out,
     deltas_out,
     panel,
     gath,
+    gath_half,
+    half,
     table,
     hist,
     inv_deg,
@@ -37,6 +42,12 @@
     deg_recv,
     tot_send,
     tot_recv,
+    inv_send,
+    inv_recv,
+    inv_split,
+    col_parts,
+    col_send,
+    col_recv,
     tile_sem,
     gs_sem,
     gr_sem,
@@ -46,6 +57,10 @@
     dr_sem,
     ts_sem,
     tr_sem,
+    is_sem,
+    ir_sem,
+    ws_sem,
+    wr_sem,
 ):
     vectors = seeds.shape[0]
     piece_blocks = seeds.shape[1] // BLOCK
@@ -166,10 +181,17 @@
         degree_copy(d).start()
     deg_recv[row] = deg_send[row]
 
+    def pieces_of(it, owner):
+        held = gath.at[it] if it < RAW_ITERS else gath_half.at[it - RAW_ITERS]
+        return held.at[pl.ds(owner * piece_blocks, piece_blocks)]
+
+    def piece_source(it):
+        return hist.at[it] if it < RAW_ITERS else half.at[it - RAW_ITERS]
+
     def own_copy(it):
-        own = gath.at[it, pl.ds(col * piece_blocks, piece_blocks)]
-        return pltpu.make_async_remote_copy(
-            src_ref=hist.at[it],
+        own = pieces_of(it, col)
+        return pltpu.make_async_remote_copy(
+            src_ref=piece_source(it),
             dst_ref=own,
             send_sem=gs_sem.at[it, 0],
             recv_sem=gr_sem.at[it, 0],
@@ -179,9 +201,9 @@
 
     def far_copy(it, d):
         to = lax.rem(z + d, chips) * 2 + core
-        own = gath.at[it, pl.ds(col * piece_blocks, piece_blocks)]
-        return pltpu.make_async_remote_copy(
-            src_ref=hist.at[it],
+        own = pieces_of(it, col)
+        return pltpu.make_async_remote_copy(
+            src_ref=piece_source(it),
             dst_ref=own,
             send_sem=gs_sem.at[it, d],
             recv_sem=gr_sem.at[it, d],
@@ -191,7 +213,7 @@
 
     def pass_copy(it, d):
         source = lax.rem(z - d + chips, chips) * 2 + core
-        there = gath.at[it, pl.ds(source * piece_blocks, piece_blocks)]
+        there = pieces_of(it, source)
         return pltpu.make_async_remote_copy(
             src_ref=there,
             dst_ref=there,
@@ -217,7 +239,7 @@
     ).astype(jnp.float32).astype(jnp.bfloat16)
 
     def fill_table(it, scale, b):
-        value = gath[it, b] * scale
+        value = gath[it, b] * scale if it < RAW_ITERS else gath_half[it - RAW_ITERS, b].astype(jnp.float32)
         table[b] = jnp.concatenate([value, value], axis=0).astype(jnp.bfloat16)
 
     def product_chunk(chunk, acc):
@@ -246,14 +268,125 @@
             worst = jnp.maximum(worst, jnp.abs(change))
         return to_row(jnp.max(worst, axis=1, keepdims=True), it * vectors)
 
+    def inverse_copy(d):
+        to = lax.rem(row + d, n_row)
+        return pltpu.make_async_remote_copy(
+            src_ref=inv_send,
+            dst_ref=inv_recv.at[pl.ds(row * piece_blocks, piece_blocks)],
+            send_sem=is_sem.at[d],
+            recv_sem=ir_sem.at[d],
+            device_id=(to, col),
+            device_id_type=MESH,
+        )
+
+    def column_copy(d):
+        to = lax.rem(col + d, n_col)
+        return pltpu.make_async_remote_copy(
+            src_ref=col_send.at[to],
+            dst_ref=col_recv.at[col],
+            send_sem=ws_sem.at[d],
+            recv_sem=wr_sem.at[d],
+            device_id=(row, to),
+            device_id_type=MESH,
+        )
+
+    def degree_inverse():
+        for d in range(1, n_row):
+            degree_copy(d).wait_recv()
+        for p in range(piece_blocks):
+            found = jnp.ones((1, BLOCK), jnp.float32)
+            for j in range(n_row):
+                for s in range(ROW_CAP):
+                    where_to = deg_recv[j, ROW_CAP + s : ROW_CAP + s + 1]
+                    found = found + jnp.where(
+                        where_to == float(p), deg_recv[j, s : s + 1], 0.0
+                    )
+            inverse = 1.0 / found
+            inv_send[p] = inverse
+            inv_deg[p] = jnp.broadcast_to(inverse, (vectors, BLOCK))
+        for d in range(1, n_row):
+            inverse_copy(d).start()
+        inv_recv[pl.ds(row * piece_blocks, piece_blocks)] = inv_send[...]
+
+    def split(value):
+        high = value.astype(jnp.bfloat16).astype(jnp.float32)
+        rest = value - high
+        middle = rest.astype(jnp.bfloat16).astype(jnp.float32)
+        return high, middle, rest - middle
+
+    def column_chunk(chunk, carry):
+        found = []
+        for t in range(CHUNK):
+            product = lax.dot_general(
+                inv_split[rows[chunk * CHUNK + t]],
+                panel[chunk, :, t * BLOCK : (t + 1) * BLOCK],
+                (((1,), (0,)), ((), ())),
+                preferred_element_type=jnp.float32,
+            )
+            found.append(jnp.sum(product, axis=0, keepdims=True))
+        col_parts[chunk] = jnp.concatenate(found, axis=0)
+        return carry
+
+    def column_parts():
+        for d in range(1, n_row):
+            inverse_copy(d).wait_recv()
+        pad = jnp.zeros((2 * vectors - 3, BLOCK), jnp.float32)
+
+        @pl.loop(0, n_row * piece_blocks, unroll=8)
+        def _(b):
+            inv_split[b] = jnp.concatenate([*split(inv_recv[b]), pad], axis=0).astype(
+                jnp.bfloat16
+            )
+
+        lax.fori_loop(0, chunks, column_chunk, 0)
+        blocks = n_col * piece_blocks
+        pick = lax.broadcasted_iota(jnp.int32, (blocks, chunks * CHUNK), 0) == live_cols[...]
+        pick = jnp.where(pick, 1.0, 0.0).astype(jnp.bfloat16)
+        held = col_parts[...].reshape(chunks * CHUNK, BLOCK)
+        gathered = jnp.zeros((blocks, BLOCK), jnp.float32)
+        for term in split(held):
+            gathered = gathered + jnp.dot(
+                pick, term.astype(jnp.bfloat16), preferred_element_type=jnp.float32
+            )
+        col_send[...] = gathered.reshape(n_col, piece_blocks, BLOCK)
+        for d in range(1, n_col):
+            column_copy(d).start()
+        col_recv[col] = col_send[col]
+
+    def share_ahead(it, scale, column_sum):
+        ahead = jnp.zeros((vectors, BLOCK), jnp.float32)
+        for b in range(piece_blocks):
+            value = hist[it, b] * scale
+            rounded = value.astype(jnp.bfloat16).astype(jnp.float32)
+            ahead = ahead + column_sum[b : b + 1] * rounded + inv_deg[b] * value
+        share(it + 1, to_row(jnp.sum(ahead, axis=1, keepdims=True)))
+
     delta_row = jnp.zeros((1, BLOCK), jnp.float32)
+    column_sum = None
     scale_before = None
     for it in range(ITERS):
+        mine = pl.ds(col * piece_blocks, piece_blocks)
+        if it >= RAW_ITERS:
+            scale = total_nodes / to_column(jnp.sum(shared(it), axis=0))
+            for b in range(piece_blocks):
+                half[it - RAW_ITERS, b] = (hist[it, b] * scale).astype(jnp.bfloat16)
         for d in range(1, chips):
             far_copy(it, d).start()
         own_copy(it).start()
-        gath[it, pl.ds(col * piece_blocks, piece_blocks)] = hist[it]
-        scale = total_nodes / to_column(jnp.sum(shared(it), axis=0))
+        if it >= RAW_ITERS:
+            gath_half[it - RAW_ITERS, mine] = half[it - RAW_ITERS]
+        else:
+            gath[it, mine] = hist[it]
+        if it == 0:
+            degree_inverse()
+        if it < RAW_ITERS:
+            scale = total_nodes / to_column(jnp.sum(shared(it), axis=0))
+        if it == 1:
+            for d in range(1, n_col):
+                column_copy(d).wait_recv()
+            column_sum = jnp.sum(col_recv[...], axis=0)
+        if it >= 1:
+            share_ahead(it, scale, column_sum)
         if it > 0:
             delta_row = delta_row + own_delta(it - 1, scale, scale_before)
         scale_before = scale
@@ -276,17 +409,7 @@
             part_copy(it, d).start()
         landed[it, row] = part[it, row]
         if it == 0:
-            for d in range(1, n_row):
-                degree_copy(d).wait_recv()
-            for p in range(piece_blocks):
-                found = jnp.ones((1, BLOCK), jnp.float32)
-                for j in range(n_row):
-                    for s in range(ROW_CAP):
-                        where_to = deg_recv[j, ROW_CAP + s : ROW_CAP + s + 1]
-                        found = found + jnp.where(
-                            where_to == float(p), deg_recv[j, s : s + 1], 0.0
-                        )
-                inv_deg[p] = jnp.broadcast_to(1.0 / found, (vectors, BLOCK))
+            column_parts()
         for d in range(1, n_row):
             part_copy(it, d).wait_recv()
         sums = [hist[it, p] * scale for p in range(piece_blocks)]
@@ -303,7 +426,8 @@
             fresh = sums[p] * inv_deg[p]
             hist[it + 1, p] = fresh
             local = local + fresh
-        share(it + 1, to_row(jnp.sum(local, axis=1, keepdims=True)))
+        if it == 0:
+            share(1, to_row(jnp.sum(local, axis=1, keepdims=True)))
 
     scale = total_nodes / to_column(jnp.sum(shared(ITERS), axis=0))
     delta_row = delta_row + own_delta(ITERS - 1, scale, scale_before)
@@ -312,6 +436,9 @@
         out[:, b * BLOCK : (b + 1) * BLOCK] = hist[ITERS, b] * scale
     for d in range(1, n_row):
         degree_copy(d).wait_send()
+        inverse_copy(d).wait_send()
+    for d in range(1, n_col):
+        column_copy(d).wait_send()
     for it in range(ITERS):
         own_copy(it).wait_send()
         for d in range(1, chips):
@@ -352,6 +479,7 @@
     match = (slot[:, None] == slot_index[None, :]) & (present[:, None] == 1)
     slot_ids = jnp.sum(jnp.where(match, (blocks % piece_blocks)[:, None], 0), axis=0)
 
+    live_cols = jnp.where(live, block_cols[0, 0], -1)[None, :]
     smem = pl.BlockSpec(memory_space=pltpu.SMEM)
     vmem = pl.BlockSpec(memory_space=pltpu.VMEM)
     f32, bf16 = jnp.float32, jnp.bfloat16
@@ -362,11 +490,13 @@
             jax.ShapeDtypeStruct(seeds.shape, f32),
             jax.ShapeDtypeStruct((ITERS, vectors), f32),
         ),
-        in_specs=[smem, smem, smem, pl.BlockSpec(memory_space=pl.ANY), vmem],
+        in_specs=[smem, smem, smem, smem, vmem, pl.BlockSpec(memory_space=pl.ANY), vmem],
         out_specs=(vmem, vmem),
         scratch_shapes=[
             pltpu.VMEM((chunks, BLOCK, CHUNK * BLOCK), bf16),
-            pltpu.VMEM((ITERS, n_col * piece_blocks, vectors, BLOCK), f32),
+            pltpu.VMEM((RAW_ITERS, n_col * piece_blocks, vectors, BLOCK), f32),
+            pltpu.VMEM((ITERS - RAW_ITERS, n_col * piece_blocks, vectors, BLOCK), bf16),
+            pltpu.VMEM((ITERS - RAW_ITERS, piece_blocks, vectors, BLOCK), bf16),
             pltpu.VMEM((n_col * piece_blocks, 2 * vectors, BLOCK), bf16),
             pltpu.VMEM((ITERS + 1, piece_blocks, vectors, BLOCK), f32),
             pltpu.VMEM((piece_blocks, vectors, BLOCK), f32),
@@ -376,6 +506,12 @@
             pltpu.VMEM((n_row, 2 * ROW_CAP, BLOCK), f32),
             pltpu.VMEM((ITERS + 2, 1, BLOCK), f32),
             pltpu.VMEM((ITERS + 2, devices, 1, BLOCK), f32),
+            pltpu.VMEM((piece_blocks, 1, BLOCK), f32),
+            pltpu.VMEM((span, 1, BLOCK), f32),
+            pltpu.VMEM((span, 2 * vectors, BLOCK), bf16),
+            pltpu.VMEM((chunks, CHUNK, BLOCK), f32),
+            pltpu.VMEM((n_col, piece_blocks, BLOCK), f32),
+            pltpu.VMEM((n_col, piece_blocks, BLOCK), f32),
             dma((chunks,)),
             dma((ITERS, n_col)),
             dma((ITERS, n_col)),
@@ -385,9 +521,13 @@
             dma((n_row,)),
             dma((ITERS + 2,)),
             dma((ITERS + 2,)),
+            dma((n_row,)),
+            dma((n_row,)),
+            dma((n_col,)),
+            dma((n_col,)),
         ],
         compiler_params=pltpu.CompilerParams(collective_id=0, has_side_effects=True),
-    )(targets, block_cols[0, 0], slot_ids, tiles, seeds)
+    )(targets, block_cols[0, 0], slot_ids, rows, live_cols, tiles, seeds)
     return out, deltas
 
 

time: 86.4 us -> 77.7 us (0.90)
  Pallas kernels: 79.5 us -> 69.4 us
  other arithmetic: 2.87 us -> 4.05 us
    pallas_call x1, Pallas kernels: 79.5 us -> 69.4 us  [on_device(): pl.pallas_call(functools.partial(kernel, n_row, n_col, float(seeds.shape[...]
    select_n x0 -> x1, other arithmetic: none -> 1.18 us  [on_device(): live_cols = jnp.where(live, block_cols[0, 0], -1)[None, :]]
where the time goes in v2:
time: 77.7 us; the launch traced here: 77.4 us
  Pallas kernels  69.4 us (89%)
  other arithmetic  4.05 us (5%)
  local copies, waits for them, and re-layouts  2.71 us (3%)
  between operations  1.31 us (2%)
    pallas_call x1, Pallas kernels, on_device(): pl.pallas_call(functools.partial(kernel, n_row, n_col, float(seeds.shape[...  69.4 us
    unnamed x2, local copies, waits for them, and re-layouts  2.71 us

profile of v2, /device:TPU:0, one launch (start us, length us, event | category | flops | bytes accessed | tf_op | source)
XLA Modules:
  0.0 77.4 jit_solution(9430936173875177048)
XLA Ops:
  1.3 0.8 convert_reduce_fusion
  2.1 1.2 %compare_select_fusion.live_cols = s32[1,128]{1,0:T(1,128)} fusion(s32[1,1,128]{2,1,0:T(1,128)} %param.7, s32[]{:T(128)} %bitcast.6), kind=kLoop, calls=%fused_computation.10 | loop fusion | flops 256 | bytes 1028 | tf_op jit(solution)/shard_map/jit(_where)/select_n | solution.py:482
  3.3 0.2 select_reduce_fusion.1
  3.5 0.6 select_reduce_fusion.2.slot_ids
  4.1 0.7 select_reduce_fusion
  4.8 0.5 broadcast_add_fusion.targets
  5.4 69.4 %shard_map.68 = (f32[8,2048]{1,0:T(8,128)}, f32[4,8]{1,0:T(4,128)}) custom-call(s32[128]{0:T(128)} %broadcast_add_fusion.targets, s32[128]{0:T(128)} %bitcast.10, s32[16]{0:T(128)} %select_reduce_fusion.2.slot_ids, s32[128]{0:T(128)} %bitcast.9, s32[1,128]{1,0:T(1,128)} %compare_select_fusion.live_cols, bf16[1,1,128,128,128]{4,3,2,1,0:T(8,128)(2,1)} %tiles.1, ...), custom_call_target="tpu_custom_call" | custom-call | tf_op jit(solution)/shard_map/pallas_call | solution.py:487
  74.7 1.5 %copy.10 = f32[8,2048]{1,0:T(8,128)} copy(f32[8,2048]{1,0:T(8,128)} %get-tuple-element.7) | data formatting | bytes 131072
  76.2 1.2 %copy.11 = f32[4,8]{1,0:T(4,128)} copy(f32[4,8]{1,0:T(4,128)} %get-tuple-element.8) | data formatting | bytes 256
  (4 shorter events, 0.0 us)
